TPU v7x, 32 devices: a whole 2x2x4 slice. The times are simulated.
32 devices in a mesh: subj: 8 (over z, y), slab: 4 (over x, core).
Axes of the slice: x: 2, y: 2, z: 4, core: 2. Of those that a mesh axis runs over, the one named last changes fastest.
Arguments:
- fod: bfloat16 [32, 45, 2048], P('subj', None, 'slab'), may hold values from -24 to 24
- rotation: bfloat16 [32, 45, 45, 2048], P('subj', None, None, 'slab'), may hold values from -0.875 to 0.875
- modulation: float32 [32, 2048], P('subj', 'slab'), may hold values from 0.3 to 3
- subject_ids: int32 [32], P('subj'), may hold values from 0 to 31, each once
- subject_weight: float32 [32], replicated, may hold values from 0.5 to 2
- voxel_cell_index: int32 [2048], P('slab'), may hold values from 0 to 1023, as said below
Outputs:
- template: bfloat16 [45, 4096], replicated
Inputs may be any that keep to these rules, and one draw needn't show every extreme that they name: `voxel_cell_index`: within each aligned block of 512 entries (one slab's masked voxels) the cell numbers are distinct and increasing.
All inputs are finite; a program needn't handle non-finite values.
Results may differ from a plain program's by a relative error of at most 0.001.
Values may be sent and summed in bfloat16 or wider, within the bound.
A program may use at most 64 MiB of HBM per device.

v0:
```python
import jax
import jax.numpy as jnp
from jax import lax
from jax.sharding import PartitionSpec as P

GRID_DEV = 1024


def on_device(fod, rotation, modulation, subject_ids, subject_weight, voxel_cell_index):
    total_subjects = subject_weight.shape[0]
    indicator_rows = (
        subject_ids[:, None] == jnp.arange(total_subjects, dtype=jnp.int32)[None, :]
    ).astype(jnp.float32)
    selected_cells = jnp.dot(indicator_rows, subject_weight, precision=lax.Precision.HIGHEST)
    weight = modulation * selected_cells[:, None]
    rotated_coefficients = jnp.einsum(
        "xfhu,xhu->xfu", rotation, fod, preferred_element_type=jnp.float32
    )
    numer = jnp.sum(rotated_coefficients * weight[:, None, :], axis=0)
    denom = jnp.sum(weight, axis=0)
    numer, denom = lax.psum((numer, denom), "subj")
    average = (numer / denom[None, :]).astype(jnp.bfloat16)
    dense = jnp.zeros((average.shape[0], GRID_DEV), jnp.bfloat16)
    dense = dense.at[:, voxel_cell_index].set(average)
    return lax.all_gather(dense, "slab", axis=1, tiled=True)


def solution(mesh):
    placed = (
        P("subj", None, "slab"),
        P("subj", None, None, "slab"),
        P("subj", "slab"),
        P("subj"),
        P(),
        P("slab"),
    )
    return jax.shard_map(on_device, mesh=mesh, in_specs=placed, out_specs=P(), check_vma=False)
```

profile of v0, /device:TPU:0, one launch (start us, length us, event | category | flops | bytes accessed | tf_op | source)
XLA Modules:
  0.0 111.8 jit_solution(3160087233603717276)
XLA Ops:
  6.5 0.0 copy-start
  6.5 0.0 copy-start.1
  6.5 0.0 all-reduce.2.cloned.1.call-start
  6.5 1.0 bitcast_convert_fusion
  7.5 0.0 copy-done
  7.5 0.8 convolution_bitcast_fusion
  8.4 0.8 fusion.5
  9.2 7.8 %multiply_reduce_fusion = f32[4,512,45]{1,0,2:T(4,128)S(1)} fusion(f32[4,512,45]{1,0,2:T(4,128)S(1)} %bitcast_convert_fusion, bf16[4,45,45,512]{3,0,2,1:T(4,128)(2,1)} %param.7), kind=kLoop, calls=%fused_computation.1 | loop fusion | flops 12349440 | bytes 9031680 | tf_op jit(solution)/shard_map/xfhu,xhu->xfu/dot_general | solution.py:16
  16.9 0.9 multiply_reduce_fusion.1
  17.8 0.0 all-reduce.2.cloned.1.call-update
  17.8 0.0 copy-done.1
  17.9 23.3 %psum.15 = f32[512]{0:T(512)S(1)} all-reduce(f32[512]{0:T(512)S(1)} %get-tuple-element.5), channel_id=1, replica_groups=mesh['subj'=8,'slab'=4] {'subj'}, use_global_device_ids=true, to_apply=%region_3.0 | all-reduce | flops 512 | bytes 4096 | tf_op jit(solution)/shard_map/psum | solution.py:21
  41.1 49.8 %all-reduce.2.cloned.1.call-done = f32[45,512]{1,0:T(8,128)} async-done(((f32[45,512]{1,0:T(8,128)}), f32[45,512]{1,0:T(8,128)}) %all-reduce.2.cloned.1.call-update) | async-done | bytes 92176 | tf_op jit(solution)/shard_map/psum | solution.py:21
  90.9 0.9 fusion.2
  91.8 0.1 copy.8
  92.0 1.8 %scatter_custom_fusion = bf16[45,1024]{0,1:T(8,128)(2,1)S(1)} fusion(s32[512]{0:T(512)S(1)} %compare_select_fusion, bf16[512,45]{1,0:T(8,128)(2,1)S(1)} %copy.8, bf16[]{:T(256)} %constant.0.clone.1), kind=kCustom, calls=%fused_computation.5 | custom fusion | bytes 92162 | tf_op jit(solution)/shard_map/scatter | solution.py:24
  93.8 10.0 %all_gather.3 = bf16[45,4096]{0,1:T(8,128)(2,1)S(1)} all-gather(bf16[45,1024]{0,1:T(8,128)(2,1)S(1)} %scatter_custom_fusion), channel_id=1, replica_groups=mesh['subj'=8,'slab'=4] {'slab'}, dimensions={1}, use_global_device_ids=true | all-gather | bytes 460800 | tf_op jit(solution)/shard_map/all_gather | solution.py:25
  103.8 1.2 %copy.9 = bf16[45,4096]{1,0:T(8,128)(2,1)} copy(bf16[45,4096]{0,1:T(8,128)(2,1)S(1)} %all_gather.3) | data formatting | bytes 737280 | tf_op jit(solution)/shard_map/all_gather | solution.py:25
  (1 shorter events, 0.0 us)
Async XLA Ops:
  6.5 1.0 copy-start
  6.5 11.3 %copy-start.1 = (s32[512]{0:T(512)S(1)}, s32[512]{0:T(512)}, u32[]{:S(2)}) copy-start(s32[512]{0:T(512)} %param.11) | copy-start | bytes 6148
  6.5 84.4 %all-reduce.2.cloned.1.call-start = ((), (), s32[]{:S(2)}) async-start(), calls=%async_computation | async-start | bytes 196608 | tf_op jit(solution)/shard_map/psum | solution.py:21
Sparse Core Ops, SparseCore 0:
  18.0 72.8 all-reduce.1
where the time goes:
time: 112 us
  waiting for transfers between devices  49.8 us (44%)
  blocking collectives  33.3 us (30%)
  between operations  13.4 us (12%)
  other arithmetic  11.3 us (10%)
  local copies, waits for them, and re-layouts  3.16 us (3%)
    psum x1, waiting for transfers between devices, on_device(): numer, denom = lax.psum((numer, denom), 'subj')  49.8 us
    psum x1, blocking collectives, on_device(): numer, denom = lax.psum((numer, denom), 'subj')  23.3 us
    all_gather x1, blocking collectives, on_device(): return lax.all_gather(dense, 'slab', axis=1, tiled=True)  10 us
    dot_general x1, other arithmetic, on_device(): jnp.einsum('xfhu,xhu->xfu', rotation, fod, preferred_element_type=jnp.flo...  7.78 us
  transfers between devices with their start and end apart: 1, of which 1 were waited for; matrix products, arithmetic and copies ran while one was open for 0% of the time, Pallas kernels for 0%

commit v1 on v0

v1 whole, which is shorter than its diff:
```python
import functools
import jax
import jax.numpy as jnp
from jax import lax
from jax.experimental import pallas as pl
from jax.experimental.pallas import tpu as pltpu
from jax.sharding import PartitionSpec as P

GRID_DEV = 1024
LANES = 128
SUBLANES = 8
UNROLL = 3
MESH = pl.DeviceIdType.MESH


def near_first(n):
    order = []
    for d in range(1, n // 2 + 1):
        order.append(d)
        if n - d != d:
            order.append(n - d)
    return order


def kernel(n, slabs, groups, rows, fod_h, rot_h, mod_h, ids_ref, sw_ref, cell_h, out_ref,
           fod_v, rot_v, mod_v, cell_v, wf, sums, part, recv, den_part, den_recv, gath, hot,
           in_sem, rot_sem, rs_send, rs_recv, dn_send, dn_recv, ix_send, ix_recv,
           a1_send, a1_recv, a2_send, a2_recv):
    coef, _, height, _ = rot_h.shape
    blocks = cell_h.shape[1] // LANES
    vox = cell_h.shape[1]
    subs = height // blocks
    me = lax.axis_index("subj")
    slab = lax.axis_index("slab")

    fod_in = pltpu.make_async_copy(fod_h, fod_v, in_sem.at[0])
    mod_in = pltpu.make_async_copy(mod_h, mod_v, in_sem.at[1])
    cell_in = pltpu.make_async_copy(cell_h, cell_v.at[slab], in_sem.at[2])
    fod_in.start()
    mod_in.start()
    chunks = []
    for i, c0 in enumerate(range(0, coef, SUBLANES)):
        span = pl.ds(c0, min(SUBLANES, coef - c0))
        chunks.append(pltpu.make_async_copy(rot_h.at[span], rot_v.at[span], rot_sem.at[i]))
        chunks[-1].start()
    cell_in.start()

    barrier = pltpu.get_barrier_semaphore()
    for d in range(1, n):
        pl.semaphore_signal(barrier, inc=1, device_id={"subj": lax.rem(me + d, n)}, device_id_type=MESH)
    for d in range(1, slabs):
        pl.semaphore_signal(barrier, inc=1, device_id={"slab": lax.rem(slab + d, slabs)}, device_id_type=MESH)

    mod_in.wait()
    row = lax.rem(lax.broadcasted_iota(jnp.int32, (height, LANES), 0), subs)
    share = jnp.zeros((height, LANES), jnp.float32)
    for s in range(subs):
        share = jnp.where(row == s, sw_ref[ids_ref[s]], share)
    w = mod_v[...] * share
    for b in range(blocks):
        den_part[b] = jnp.sum(w[b * subs:(b + 1) * subs], axis=0, keepdims=True)
    fod_in.wait()
    wf[...] = fod_v[...].astype(jnp.float32) * w[None]

    def copy_to(src, dst, send, rec, where):
        return pltpu.make_async_remote_copy(
            src_ref=src, dst_ref=dst, send_sem=send, recv_sem=rec,
            device_id=where, device_id_type=MESH)

    def piece_copy(i, g):
        dest = lax.rem(me // groups + i, blocks) * groups + g
        return dest, copy_to(part.at[dest], recv.at[me], rs_send.at[i * groups + g],
                             rs_recv.at[me], {"subj": dest})

    per = rows // SUBLANES
    for g in range(groups):
        for q in range(per):
            base = g * rows + q * SUBLANES
            count = max(0, min(SUBLANES, coef - base))
            if count:
                chunks[base // SUBLANES].wait()

            def step(k, accs):
                factor = wf[k]
                return tuple(acc + rot_v[base + r, k].astype(jnp.float32) * factor
                             for r, acc in enumerate(accs))

            zero = jnp.zeros((height, LANES), jnp.float32)
            if count:
                accs = lax.fori_loop(0, coef, step, (zero,) * count, unroll=UNROLL)
            else:
                accs = ()
            for r in range(SUBLANES):
                sums[q % 2, pl.ds(r * height, height), :] = accs[r] if r < count else zero
            for b in range(blocks):
                tile = None
                for s in range(subs):
                    line = sums[q % 2, pl.ds(b * subs + s, SUBLANES, stride=height), :]
                    tile = line if tile is None else tile + line
                part[b * groups + g, pl.ds(q * SUBLANES, SUBLANES), :] = tile
        if g == 0:
            pl.semaphore_wait(barrier, n + slabs - 2)
        for i in range(blocks):
            dest, copy = piece_copy(i, g)

            @pl.when(dest != me)
            def _():
                copy.start()
        if g == 0:
            for d in range(1, n):
                dest = lax.rem(me + d, n)
                copy_to(den_part.at[dest // groups], den_recv.at[me], dn_send.at[d],
                        dn_recv.at[me], {"subj": dest}).start()
            cell_in.wait()
            for d in range(1, slabs):
                copy_to(cell_v.at[slab], cell_v.at[slab], ix_send.at[d],
                        ix_recv.at[slab], {"slab": lax.rem(slab + d, slabs)}).start()

    def make_hot(p):
        cells = jnp.transpose(jnp.broadcast_to(cell_v[p].astype(jnp.float32), (LANES, vox)))
        lane = lax.broadcasted_iota(jnp.int32, (vox, LANES), 1).astype(jnp.float32)
        for k in range(GRID_DEV // LANES):
            hit = jnp.where(cells == lane + float(k * LANES), 1.0, 0.0)
            hot[p, :, k * LANES:(k + 1) * LANES] = hit.astype(jnp.bfloat16)

    make_hot(slab)

    den = den_part[me // groups]
    for d in near_first(n):
        src = lax.rem(me + d, n)
        copy_to(den_part.at[0], den_recv.at[src], dn_send.at[d], dn_recv.at[src], {"subj": src}).wait_recv()
        den = den + den_recv[src]
    acc = part[me]
    for d in near_first(n):
        src = lax.rem(me + d, n)
        copy_to(part.at[0], recv.at[src], rs_send.at[0], rs_recv.at[src], {"subj": src}).wait_recv()
        acc = acc + recv[src]
    average = (acc / den).reshape(per, SUBLANES, LANES).astype(jnp.bfloat16)
    gath[slab, me] = average

    def forward(d, j):
        peer = lax.rem(slab + d, slabs)
        return copy_to(gath.at[slab, j], gath.at[slab, j], a2_send.at[d, j], a2_recv.at[slab, j],
                       {"slab": peer})

    def first(d):
        return copy_to(gath.at[slab, me], gath.at[slab, me], a1_send.at[d], a1_recv.at[me],
                       {"subj": lax.rem(me + d, n)})

    for d in near_first(n)[::-1]:
        first(d).start()
    for d in range(1, slabs):
        forward(d, me).start()

    for d in range(1, slabs):
        p = lax.rem(slab + d, slabs)
        copy_to(cell_v.at[slab], cell_v.at[p], ix_send.at[d], ix_recv.at[p], {"slab": p}).wait_recv()
        make_hot(p)

    for k in near_first(n):
        src = lax.rem(me + k, n)
        copy_to(gath.at[slab, me], gath.at[slab, src], a1_send.at[k], a1_recv.at[src], {"subj": src}).wait_recv()
        for d in range(1, slabs):
            forward(d, src).start()

    def place(p):
        lines = []
        for g in range(groups):
            cols = [gath[p, b * groups + g].astype(jnp.float32).reshape(rows, LANES) for b in range(blocks)]
            lines.append(jnp.concatenate(cols, axis=1))
        dense = jnp.concatenate(lines, axis=0).astype(jnp.bfloat16)
        placed = jnp.dot(dense, hot[p], preferred_element_type=jnp.float32)
        at = pl.ds(pl.multiple_of(p * GRID_DEV, GRID_DEV), GRID_DEV)
        out_ref[:, at] = placed[:coef].astype(jnp.bfloat16)

    place(slab)
    for d in range(1, slabs):
        p = lax.rem(slab + d, slabs)
        for j in range(n):
            copy_to(gath.at[slab, j], gath.at[p, j], a2_send.at[d, j], a2_recv.at[p, j], {"slab": p}).wait_recv()
        place(p)

    for g in range(groups):
        for i in range(blocks):
            dest, copy = piece_copy(i, g)

            @pl.when(dest != me)
            def _():
                copy.wait_send()
    for d in range(1, n):
        copy_to(den_part.at[0], den_recv.at[me], dn_send.at[d], dn_recv.at[me],
                {"subj": lax.rem(me + d, n)}).wait_send()
        first(d).wait_send()
    for d in range(1, slabs):
        copy_to(cell_v.at[slab], cell_v.at[slab], ix_send.at[d], ix_recv.at[slab],
                {"slab": lax.rem(slab + d, slabs)}).wait_send()
        for j in range(n):
            forward(d, j).wait_send()


def on_device(n, slabs, fod, rotation, modulation, subject_ids, subject_weight, voxel_cell_index):
    subs, coef, _, vox = rotation.shape
    blocks = vox // LANES
    assert vox % LANES == 0 and n % blocks == 0
    groups = n // blocks
    rows = -(-(-(-coef // groups)) // SUBLANES) * SUBLANES
    per = rows // SUBLANES
    height = blocks * subs
    rot_rows = rotation.reshape(subs, coef, coef, blocks, LANES).transpose(1, 2, 3, 0, 4)
    rot_rows = rot_rows.reshape(coef, coef, height, LANES)
    fod_rows = fod.reshape(subs, coef, blocks, LANES).transpose(1, 2, 0, 3).reshape(coef, height, LANES)
    mod_rows = modulation.reshape(subs, blocks, LANES).transpose(1, 0, 2).reshape(height, LANES)
    dma = pltpu.SemaphoreType.DMA
    anywhere = pl.BlockSpec(memory_space=pl.ANY)
    smem = pl.BlockSpec(memory_space=pltpu.SMEM)
    return pl.pallas_call(
        functools.partial(kernel, n, slabs, groups, rows),
        out_shape=jax.ShapeDtypeStruct((coef, slabs * GRID_DEV), jnp.bfloat16),
        in_specs=[anywhere, anywhere, anywhere, smem, smem, anywhere],
        out_specs=pl.BlockSpec(memory_space=pltpu.VMEM),
        scratch_shapes=[
            pltpu.VMEM((coef, height, LANES), jnp.bfloat16),
            pltpu.VMEM((coef, coef, height, LANES), jnp.bfloat16),
            pltpu.VMEM((height, LANES), jnp.float32),
            pltpu.VMEM((slabs, 1, vox), jnp.int32),
            pltpu.VMEM((coef, height, LANES), jnp.float32),
            pltpu.VMEM((2, SUBLANES * height, LANES), jnp.float32),
            pltpu.VMEM((n, rows, LANES), jnp.float32),
            pltpu.VMEM((n, rows, LANES), jnp.float32),
            pltpu.VMEM((blocks, 1, LANES), jnp.float32),
            pltpu.VMEM((n, 1, LANES), jnp.float32),
            pltpu.VMEM((slabs, n, per, SUBLANES, LANES), jnp.bfloat16),
            pltpu.VMEM((slabs, vox, GRID_DEV), jnp.bfloat16),
            dma((3,)),
            dma((-(-coef // SUBLANES),)),
            dma((n,)), dma((n,)),
            dma((n,)), dma((n,)),
            dma((slabs,)), dma((slabs,)),
            dma((n,)), dma((n,)),
            dma((slabs, n)), dma((slabs, n)),
        ],
        compiler_params=pltpu.CompilerParams(collective_id=0, has_side_effects=True),
        name="template",
    )(fod_rows, rot_rows, mod_rows, subject_ids, subject_weight, voxel_cell_index.reshape(1, vox))


def solution(mesh):
    placed = (
        P("subj", None, "slab"),
        P("subj", None, None, "slab"),
        P("subj", "slab"),
        P("subj"),
        P(),
        P("slab"),
    )
    body = functools.partial(on_device, mesh.shape["subj"], mesh.shape["slab"])
    return jax.shard_map(body, mesh=mesh, in_specs=placed, out_specs=P(), check_vma=False)
```

time: 112 us -> 24.6 us (0.22)
  waiting for transfers between devices: 49.8 us -> 0 us
  blocking collectives: 33.3 us -> 0 us
  Pallas kernels: 0 us -> 22.7 us
  between operations: 13.4 us -> 0.01 us
  other arithmetic: 11.3 us -> 0 us
  local copies, waits for them, and re-layouts: 3.16 us -> 1.77 us
    psum x1 -> x0, waiting for transfers between devices: 49.8 us -> none  [on_device(): numer, denom = lax.psum((numer, denom), 'subj')]
    psum x1 -> x0, blocking collectives: 23.3 us -> none  [on_device(): numer, denom = lax.psum((numer, denom), 'subj')]
    pallas_call x0 -> x1, Pallas kernels: none -> 22.7 us  [on_device(): pl.pallas_call(functools.partial(kernel, n, slabs, groups, rows), out_sha...]
    all_gather x1 -> x0, blocking collectives: 10 us -> none  [on_device(): return lax.all_gather(dense, 'slab', axis=1, tiled=True)]
    dot_general x1 -> x0, other arithmetic: 7.78 us -> none  [on_device(): jnp.einsum('xfhu,xhu->xfu', rotation, fod, preferred_element_type=jnp.flo...]
    scatter x1 -> x0, local copies, waits for them, and re-layouts: 1.83 us -> none  [on_device(): dense = dense.at[:, voxel_cell_index].set(average)]
    unnamed x4 -> x1, local copies, waits for them, and re-layouts: 0.01 us -> 1.77 us
    reduce_sum x2 -> x0, other arithmetic: 1.67 us -> none  [the longest x1 0.88 us: on_device(): numer = jnp.sum(rotated_coefficients * weight[:, None, :], axis=0)]
  transfers between devices with their start and end apart: 1 -> 0, of which waited for: 1 -> 0; matrix products, arithmetic and copies ran while one was open for 0% -> 0% of each run, Pallas kernels for 0% -> 0%
where the time goes in v1:
time: 24.6 us; the launch traced here: 24.4 us
  Pallas kernels  22.7 us (92%)
  local copies, waits for them, and re-layouts  1.77 us (7%)
    pallas_call x1, Pallas kernels, on_device(): pl.pallas_call(functools.partial(kernel, n, slabs, groups, rows), out_sha...  22.7 us
    unnamed x1, local copies, waits for them, and re-layouts  1.77 us

profile of v1, /device:TPU:0, one launch (start us, length us, event | category | flops | bytes accessed | tf_op | source)
XLA Modules:
  0.0 24.4 jit_solution(9606590832628772081)
XLA Ops:
  0.0 22.7 %template.1 = bf16[45,4096]{1,0:T(8,128)(2,1)} custom-call(bf16[45,16,128]{2,1,0:T(8,128)(2,1)} %bitcast.17, bf16[45,45,16,128]{3,2,1,0:T(8,128)(2,1)} %bitcast.16, f32[16,128]{1,0:T(8,128)} %bitcast.18, s32[4]{0:T(128)} %ids_ref.1, f32[32]{0:T(128)} %sw_ref.1, s32[1,512]{1,0:T(1,128)} %bitcast.19), custom_call_target="tpu_custom_call" | custom-call | tf_op jit(solution)/shard_map/template/pallas_call | solution.py:216
  22.7 1.8 %copy.11 = bf16[45,4096]{1,0:T(8,128)(2,1)} copy(bf16[45,4096]{1,0:T(8,128)(2,1)} %template.1) | data formatting | bytes 737280

commit v2 on v1

--- a/solution.py
+++ b/solution.py
@@ -10,6 +10,7 @@
 LANES = 128
 SUBLANES = 8
 UNROLL = 3
+AHEAD = 3
 MESH = pl.DeviceIdType.MESH
 
 
@@ -42,7 +43,8 @@
     for i, c0 in enumerate(range(0, coef, SUBLANES)):
         span = pl.ds(c0, min(SUBLANES, coef - c0))
         chunks.append(pltpu.make_async_copy(rot_h.at[span], rot_v.at[span], rot_sem.at[i]))
-        chunks[-1].start()
+    for chunk in chunks[:AHEAD]:
+        chunk.start()
     cell_in.start()
 
     barrier = pltpu.get_barrier_semaphore()
@@ -51,6 +53,8 @@
     for d in range(1, slabs):
         pl.semaphore_signal(barrier, inc=1, device_id={"slab": lax.rem(slab + d, slabs)}, device_id_type=MESH)
 
+    fod_in.wait()
+    wf[...] = fod_v[...].astype(jnp.float32)
     mod_in.wait()
     row = lax.rem(lax.broadcasted_iota(jnp.int32, (height, LANES), 0), subs)
     share = jnp.zeros((height, LANES), jnp.float32)
@@ -59,8 +63,6 @@
     w = mod_v[...] * share
     for b in range(blocks):
         den_part[b] = jnp.sum(w[b * subs:(b + 1) * subs], axis=0, keepdims=True)
-    fod_in.wait()
-    wf[...] = fod_v[...].astype(jnp.float32) * w[None]
 
     def copy_to(src, dst, send, rec, where):
         return pltpu.make_async_remote_copy(
@@ -78,7 +80,10 @@
             base = g * rows + q * SUBLANES
             count = max(0, min(SUBLANES, coef - base))
             if count:
-                chunks[base // SUBLANES].wait()
+                here = base // SUBLANES
+                chunks[here].wait()
+                if here + AHEAD < len(chunks):
+                    chunks[here + AHEAD].start()
 
             def step(k, accs):
                 factor = wf[k]
@@ -91,7 +96,7 @@
             else:
                 accs = ()
             for r in range(SUBLANES):
-                sums[q % 2, pl.ds(r * height, height), :] = accs[r] if r < count else zero
+                sums[q % 2, pl.ds(r * height, height), :] = accs[r] * w if r < count else zero
             for b in range(blocks):
                 tile = None
                 for s in range(subs):
@@ -124,6 +129,10 @@
             hot[p, :, k * LANES:(k + 1) * LANES] = hit.astype(jnp.bfloat16)
 
     make_hot(slab)
+    for d in range(1, slabs):
+        p = lax.rem(slab + d, slabs)
+        copy_to(cell_v.at[slab], cell_v.at[p], ix_send.at[d], ix_recv.at[p], {"slab": p}).wait_recv()
+        make_hot(p)
 
     den = den_part[me // groups]
     for d in near_first(n):
@@ -138,10 +147,13 @@
     average = (acc / den).reshape(per, SUBLANES, LANES).astype(jnp.bfloat16)
     gath[slab, me] = average
 
-    def forward(d, j):
-        peer = lax.rem(slab + d, slabs)
-        return copy_to(gath.at[slab, j], gath.at[slab, j], a2_send.at[d, j], a2_recv.at[slab, j],
-                       {"slab": peer})
+    half = n // 2
+    near = me // half
+
+    def relay(d, side, h):
+        rows_of = gath.at[slab, pl.ds(h * half, half)]
+        return copy_to(rows_of, rows_of, a2_send.at[d, side], a2_recv.at[slab, h],
+                       {"slab": lax.rem(slab + d, slabs)})
 
     def first(d):
         return copy_to(gath.at[slab, me], gath.at[slab, me], a1_send.at[d], a1_recv.at[me],
@@ -149,19 +161,18 @@
 
     for d in near_first(n)[::-1]:
         first(d).start()
-    for d in range(1, slabs):
-        forward(d, me).start()
-
-    for d in range(1, slabs):
-        p = lax.rem(slab + d, slabs)
-        copy_to(cell_v.at[slab], cell_v.at[p], ix_send.at[d], ix_recv.at[p], {"slab": p}).wait_recv()
-        make_hot(p)
-
-    for k in near_first(n):
-        src = lax.rem(me + k, n)
-        copy_to(gath.at[slab, me], gath.at[slab, src], a1_send.at[k], a1_recv.at[src], {"subj": src}).wait_recv()
-        for d in range(1, slabs):
-            forward(d, src).start()
+
+    def arrived(src):
+        copy_to(gath.at[slab, me], gath.at[slab, src], a1_send.at[0], a1_recv.at[src], {"subj": src}).wait_recv()
+
+    for k in range(1, half):
+        arrived(near * half + lax.rem(me + k, half))
+    for d in range(1, slabs):
+        relay(d, 0, near).start()
+    for k in range(half):
+        arrived((1 - near) * half + lax.rem(me + k, half))
+    for d in range(1, slabs):
+        relay(d, 1, 1 - near).start()
 
     def place(p):
         lines = []
@@ -176,8 +187,9 @@
     place(slab)
     for d in range(1, slabs):
         p = lax.rem(slab + d, slabs)
-        for j in range(n):
-            copy_to(gath.at[slab, j], gath.at[p, j], a2_send.at[d, j], a2_recv.at[p, j], {"slab": p}).wait_recv()
+        for h in range(2):
+            rows_of = gath.at[p, pl.ds(h * half, half)]
+            copy_to(gath.at[slab, pl.ds(0, half)], rows_of, a2_send.at[d, 0], a2_recv.at[p, h], {"slab": p}).wait_recv()
         place(p)
 
     for g in range(groups):
@@ -194,14 +206,14 @@
     for d in range(1, slabs):
         copy_to(cell_v.at[slab], cell_v.at[slab], ix_send.at[d], ix_recv.at[slab],
                 {"slab": lax.rem(slab + d, slabs)}).wait_send()
-        for j in range(n):
-            forward(d, j).wait_send()
+        relay(d, 0, near).wait_send()
+        relay(d, 1, 1 - near).wait_send()
 
 
 def on_device(n, slabs, fod, rotation, modulation, subject_ids, subject_weight, voxel_cell_index):
     subs, coef, _, vox = rotation.shape
     blocks = vox // LANES
-    assert vox % LANES == 0 and n % blocks == 0
+    assert vox % LANES == 0 and n % blocks == 0 and n % 2 == 0
     groups = n // blocks
     rows = -(-(-(-coef // groups)) // SUBLANES) * SUBLANES
     per = rows // SUBLANES
@@ -211,11 +223,11 @@
     fod_rows = fod.reshape(subs, coef, blocks, LANES).transpose(1, 2, 0, 3).reshape(coef, height, LANES)
     mod_rows = modulation.reshape(subs, blocks, LANES).transpose(1, 0, 2).reshape(height, LANES)
     dma = pltpu.SemaphoreType.DMA
-    anywhere = pl.BlockSpec(memory_space=pl.ANY)
+    anywhere = pl.BlockSpec(memory_space=pltpu.HBM)
     smem = pl.BlockSpec(memory_space=pltpu.SMEM)
     return pl.pallas_call(
         functools.partial(kernel, n, slabs, groups, rows),
-        out_shape=jax.ShapeDtypeStruct((coef, slabs * GRID_DEV), jnp.bfloat16),
+        out_shape=pltpu.VMEM((coef, slabs * GRID_DEV), jnp.bfloat16),
         in_specs=[anywhere, anywhere, anywhere, smem, smem, anywhere],
         out_specs=pl.BlockSpec(memory_space=pltpu.VMEM),
         scratch_shapes=[
@@ -237,7 +249,7 @@
             dma((n,)), dma((n,)),
             dma((slabs,)), dma((slabs,)),
             dma((n,)), dma((n,)),
-            dma((slabs, n)), dma((slabs, n)),
+            dma((slabs, 2)), dma((slabs, 2)),
         ],
         compiler_params=pltpu.CompilerParams(collective_id=0, has_side_effects=True),
         name="template",

time: 24.6 us -> 21.9 us (0.89)
  Pallas kernels: 22.7 us -> 21 us
  local copies, waits for them, and re-layouts: 1.77 us -> 0.75 us
    pallas_call x1, Pallas kernels: 22.7 us -> 21 us  [on_device(): pl.pallas_call(functools.partial(kernel, n, slabs, groups, rows), out_sha...]
    unnamed x1, local copies, waits for them, and re-layouts: 1.77 us -> 0.75 us
where the time goes in v2:
time: 21.9 us; the launch traced here: 21.8 us
  Pallas kernels  21 us (96%)
  local copies, waits for them, and re-layouts  0.75 us (3%)
    pallas_call x1, Pallas kernels, on_device(): pl.pallas_call(functools.partial(kernel, n, slabs, groups, rows), out_sha...  21 us
    unnamed x1, local copies, waits for them, and re-layouts  0.75 us

profile of v2, /device:TPU:0, one launch (start us, length us, event | category | flops | bytes accessed | tf_op | source)
XLA Modules:
  0.0 21.8 jit_solution(10637901098105020166)
XLA Ops:
  0.0 21.0 %template.1 = bf16[45,4096]{1,0:T(8,128)(2,1)S(1)} custom-call(bf16[45,16,128]{2,1,0:T(8,128)(2,1)} %bitcast.17, bf16[45,45,16,128]{3,2,1,0:T(8,128)(2,1)} %bitcast.16, f32[16,128]{1,0:T(8,128)} %bitcast.18, s32[4]{0:T(128)} %ids_ref.1, f32[32]{0:T(128)} %sw_ref.1, s32[1,512]{1,0:T(1,128)} %bitcast.19), custom_call_target="tpu_custom_call" | custom-call | tf_op jit(solution)/shard_map/template/pallas_call | solution.py:228
  21.0 0.7 %copy.11 = bf16[45,4096]{1,0:T(8,128)(2,1)} copy(bf16[45,4096]{1,0:T(8,128)(2,1)S(1)} %template.1) | data formatting | bytes 737280

commit v3 on v2

--- a/solution.py
+++ b/solution.py
@@ -10,7 +10,7 @@
 LANES = 128
 SUBLANES = 8
 UNROLL = 3
-AHEAD = 3
+AHEAD = 4
 MESH = pl.DeviceIdType.MESH
 
 
@@ -23,8 +23,8 @@
     return order
 
 
-def kernel(n, slabs, groups, rows, fod_h, rot_h, mod_h, ids_ref, sw_ref, cell_h, out_ref,
-           fod_v, rot_v, mod_v, cell_v, wf, sums, part, recv, den_part, den_recv, gath, hot,
+def kernel(n, slabs, groups, rows, fod_h, rot_h, mod_h, ids_h, sw_h, cell_h, out_ref,
+           ids_ref, sw_ref, fod_v, rot_v, mod_v, cell_v, wf, sums, part, recv, den_part, den_recv, gath, hot,
            in_sem, rot_sem, rs_send, rs_recv, dn_send, dn_recv, ix_send, ix_recv,
            a1_send, a1_recv, a2_send, a2_recv):
     coef, _, height, _ = rot_h.shape
@@ -39,6 +39,10 @@
     cell_in = pltpu.make_async_copy(cell_h, cell_v.at[slab], in_sem.at[2])
     fod_in.start()
     mod_in.start()
+    ids_in = pltpu.make_async_copy(ids_h, ids_ref, in_sem.at[3])
+    sw_in = pltpu.make_async_copy(sw_h, sw_ref, in_sem.at[4])
+    ids_in.start()
+    sw_in.start()
     chunks = []
     for i, c0 in enumerate(range(0, coef, SUBLANES)):
         span = pl.ds(c0, min(SUBLANES, coef - c0))
@@ -56,6 +60,8 @@
     fod_in.wait()
     wf[...] = fod_v[...].astype(jnp.float32)
     mod_in.wait()
+    ids_in.wait()
+    sw_in.wait()
     row = lax.rem(lax.broadcasted_iota(jnp.int32, (height, LANES), 0), subs)
     share = jnp.zeros((height, LANES), jnp.float32)
     for s in range(subs):
@@ -121,17 +127,26 @@
                 copy_to(cell_v.at[slab], cell_v.at[slab], ix_send.at[d],
                         ix_recv.at[slab], {"slab": lax.rem(slab + d, slabs)}).start()
 
+    part_vox = vox // 2
+    reach = GRID_DEV - part_vox
+
     def make_hot(p):
-        cells = jnp.transpose(jnp.broadcast_to(cell_v[p].astype(jnp.float32), (LANES, vox)))
-        lane = lax.broadcasted_iota(jnp.int32, (vox, LANES), 1).astype(jnp.float32)
-        for k in range(GRID_DEV // LANES):
-            hit = jnp.where(cells == lane + float(k * LANES), 1.0, 0.0)
-            hot[p, :, k * LANES:(k + 1) * LANES] = hit.astype(jnp.bfloat16)
+        for h in range(2):
+            mine = cell_v[p, :, h * part_vox:(h + 1) * part_vox].astype(jnp.float32)
+            cells = jnp.transpose(jnp.broadcast_to(mine, (LANES, part_vox)))
+            lane = lax.broadcasted_iota(jnp.int32, (part_vox, LANES), 1).astype(jnp.float32)
+            for k in range(reach // LANES):
+                hit = jnp.where(cells == lane + float(h * part_vox + k * LANES), 1.0, 0.0)
+                hot[p, h, :, k * LANES:(k + 1) * LANES] = hit.astype(jnp.bfloat16)
+
+    out_ref[...] = jnp.zeros_like(out_ref)
+    pairs = slabs // 2
+    peers = [lax.rem(slab // 2 + dp, pairs) * 2 + lax.rem(slab + dc, 2)
+             for dp in range(pairs) for dc in range(2)][1:]
 
     make_hot(slab)
-    for d in range(1, slabs):
-        p = lax.rem(slab + d, slabs)
-        copy_to(cell_v.at[slab], cell_v.at[p], ix_send.at[d], ix_recv.at[p], {"slab": p}).wait_recv()
+    for p in peers:
+        copy_to(cell_v.at[slab], cell_v.at[p], ix_send.at[0], ix_recv.at[p], {"slab": p}).wait_recv()
         make_hot(p)
 
     den = den_part[me // groups]
@@ -150,10 +165,20 @@
     half = n // 2
     near = me // half
 
-    def relay(d, side, h):
-        rows_of = gath.at[slab, pl.ds(h * half, half)]
-        return copy_to(rows_of, rows_of, a2_send.at[d, side], a2_recv.at[slab, h],
-                       {"slab": lax.rem(slab + d, slabs)})
+    quarter = half // 2
+    far = 1 - near
+    spans = [(near * half, half), (far * half + near * quarter, quarter),
+             (far * half + far * quarter, quarter)]
+
+    def relay(i, k):
+        start, count = spans[k]
+        rows_of = gath.at[slab, pl.ds(start, count)]
+        return copy_to(rows_of, rows_of, a2_send.at[i, k], a2_recv.at[slab, k], {"slab": peers[i]})
+
+    def relayed(i, k):
+        start, count = spans[k]
+        copy_to(gath.at[slab, pl.ds(start, count)], gath.at[peers[i], pl.ds(start, count)],
+                a2_send.at[i, k], a2_recv.at[peers[i], k], {"slab": peers[i]}).wait_recv()
 
     def first(d):
         return copy_to(gath.at[slab, me], gath.at[slab, me], a1_send.at[d], a1_recv.at[me],
@@ -165,32 +190,33 @@
     def arrived(src):
         copy_to(gath.at[slab, me], gath.at[slab, src], a1_send.at[0], a1_recv.at[src], {"subj": src}).wait_recv()
 
-    for k in range(1, half):
-        arrived(near * half + lax.rem(me + k, half))
-    for d in range(1, slabs):
-        relay(d, 0, near).start()
-    for k in range(half):
-        arrived((1 - near) * half + lax.rem(me + k, half))
-    for d in range(1, slabs):
-        relay(d, 1, 1 - near).start()
-
-    def place(p):
+    def place(p, h):
         lines = []
         for g in range(groups):
-            cols = [gath[p, b * groups + g].astype(jnp.float32).reshape(rows, LANES) for b in range(blocks)]
+            cols = [gath[p, h * half + b * groups + g].astype(jnp.float32).reshape(rows, LANES)
+                    for b in range(blocks // 2)]
             lines.append(jnp.concatenate(cols, axis=1))
         dense = jnp.concatenate(lines, axis=0).astype(jnp.bfloat16)
-        placed = jnp.dot(dense, hot[p], preferred_element_type=jnp.float32)
-        at = pl.ds(pl.multiple_of(p * GRID_DEV, GRID_DEV), GRID_DEV)
-        out_ref[:, at] = placed[:coef].astype(jnp.bfloat16)
-
-    place(slab)
-    for d in range(1, slabs):
-        p = lax.rem(slab + d, slabs)
-        for h in range(2):
-            rows_of = gath.at[p, pl.ds(h * half, half)]
-            copy_to(gath.at[slab, pl.ds(0, half)], rows_of, a2_send.at[d, 0], a2_recv.at[p, h], {"slab": p}).wait_recv()
-        place(p)
+        placed = jnp.dot(dense, hot[p, h], preferred_element_type=jnp.float32)
+        at = pl.ds(pl.multiple_of(p * GRID_DEV + h * part_vox, LANES), reach)
+        held = out_ref[:, at].astype(jnp.float32)
+        out_ref[:, at] = (held + placed[:coef]).astype(jnp.bfloat16)
+
+    order = list(range(1, slabs - 1)) + [0]
+    for k in range(3):
+        start, count = spans[k]
+        for i in range(1 if k == 0 else 0, count):
+            arrived(near * half + lax.rem(me + i, half) if k == 0 else start + i)
+        for i in order:
+            relay(i, k).start()
+        if k == 0:
+            place(slab, near)
+    place(slab, far)
+    for h, ks in ((near, (0,)), (far, (1, 2))):
+        for i in range(slabs - 1):
+            for k in ks:
+                relayed(i, k)
+            place(peers[i], h)
 
     for g in range(groups):
         for i in range(blocks):
@@ -206,14 +232,14 @@
     for d in range(1, slabs):
         copy_to(cell_v.at[slab], cell_v.at[slab], ix_send.at[d], ix_recv.at[slab],
                 {"slab": lax.rem(slab + d, slabs)}).wait_send()
-        relay(d, 0, near).wait_send()
-        relay(d, 1, 1 - near).wait_send()
+        for k in range(3):
+            relay(d - 1, k).wait_send()
 
 
 def on_device(n, slabs, fod, rotation, modulation, subject_ids, subject_weight, voxel_cell_index):
     subs, coef, _, vox = rotation.shape
     blocks = vox // LANES
-    assert vox % LANES == 0 and n % blocks == 0 and n % 2 == 0
+    assert vox % LANES == 0 and n % blocks == 0 and n % 4 == 0 and blocks % 2 == 0 and slabs % 2 == 0
     groups = n // blocks
     rows = -(-(-(-coef // groups)) // SUBLANES) * SUBLANES
     per = rows // SUBLANES
@@ -224,13 +250,14 @@
     mod_rows = modulation.reshape(subs, blocks, LANES).transpose(1, 0, 2).reshape(height, LANES)
     dma = pltpu.SemaphoreType.DMA
     anywhere = pl.BlockSpec(memory_space=pltpu.HBM)
-    smem = pl.BlockSpec(memory_space=pltpu.SMEM)
     return pl.pallas_call(
         functools.partial(kernel, n, slabs, groups, rows),
         out_shape=pltpu.VMEM((coef, slabs * GRID_DEV), jnp.bfloat16),
-        in_specs=[anywhere, anywhere, anywhere, smem, smem, anywhere],
+        in_specs=[anywhere] * 6,
         out_specs=pl.BlockSpec(memory_space=pltpu.VMEM),
         scratch_shapes=[
+            pltpu.SMEM(subject_ids.shape, jnp.int32),
+            pltpu.SMEM(subject_weight.shape, jnp.float32),
             pltpu.VMEM((coef, height, LANES), jnp.bfloat16),
             pltpu.VMEM((coef, coef, height, LANES), jnp.bfloat16),
             pltpu.VMEM((height, LANES), jnp.float32),
@@ -242,14 +269,14 @@
             pltpu.VMEM((blocks, 1, LANES), jnp.float32),
             pltpu.VMEM((n, 1, LANES), jnp.float32),
             pltpu.VMEM((slabs, n, per, SUBLANES, LANES), jnp.bfloat16),
-            pltpu.VMEM((slabs, vox, GRID_DEV), jnp.bfloat16),
-            dma((3,)),
+            pltpu.VMEM((slabs, 2, vox // 2, GRID_DEV - vox // 2), jnp.bfloat16),
+            dma((5,)),
             dma((-(-coef // SUBLANES),)),
             dma((n,)), dma((n,)),
             dma((n,)), dma((n,)),
             dma((slabs,)), dma((slabs,)),
             dma((n,)), dma((n,)),
-            dma((slabs, 2)), dma((slabs, 2)),
+            dma((slabs, 3)), dma((slabs, 3)),
         ],
         compiler_params=pltpu.CompilerParams(collective_id=0, has_side_effects=True),
         name="template",

time: 21.9 us -> 21 us (0.959)
  Pallas kernels: 21 us -> 20.1 us
    pallas_call x1, Pallas kernels: 21 us -> 20.1 us  [on_device(): pl.pallas_call(functools.partial(kernel, n, slabs, groups, rows), out_sha...]
where the time goes in v3:
time: 21 us; the launch traced here: 20.9 us
  Pallas kernels  20.1 us (96%)
  local copies, waits for them, and re-layouts  0.75 us (4%)
    pallas_call x1, Pallas kernels, on_device(): pl.pallas_call(functools.partial(kernel, n, slabs, groups, rows), out_sha...  20.1 us
    unnamed x1, local copies, waits for them, and re-layouts  0.75 us

profile of v3, /device:TPU:0, one launch (start us, length us, event | category | flops | bytes accessed | tf_op | source)
XLA Modules:
  0.0 20.9 jit_solution(9388501293227333736)
XLA Ops:
  0.0 20.1 %template.1 = bf16[45,4096]{1,0:T(8,128)(2,1)S(1)} custom-call(bf16[45,16,128]{2,1,0:T(8,128)(2,1)} %bitcast.17, bf16[45,45,16,128]{3,2,1,0:T(8,128)(2,1)} %bitcast.16, f32[16,128]{1,0:T(8,128)} %bitcast.18, s32[4]{0:T(128)} %ids_h.1, f32[32]{0:T(128)} %sw_h.1, s32[1,512]{1,0:T(1,128)} %bitcast.19), custom_call_target="tpu_custom_call" | custom-call | tf_op jit(solution)/shard_map/template/pallas_call | solution.py:253
  20.1 0.7 %copy.11 = bf16[45,4096]{1,0:T(8,128)(2,1)} copy(bf16[45,4096]{1,0:T(8,128)(2,1)S(1)} %template.1) | data formatting | bytes 737280
